TPU v7x, 128 devices: a whole 4x4x4 slice. The times are simulated.
128 devices in a mesh: section: 8 (over z, x_lo), dp: 16 (over x_hi, y, core).
Axes of the slice: x: 4 (x_hi: 2, x_lo: 2; x = x_hi * 2 + x_lo), y: 4, z: 4, core: 2. Of those that a mesh axis runs over, the one named last changes fastest.
Arguments:
- acts: bfloat16 [8, 6144, 8192], P('section', 'dp'), may hold values from -6 to 6
- input_grads: bfloat16 [8, 6144, 5120], P('section', 'dp'), may hold values from -6 to 6
- head_grads: bfloat16 [6144, 5120], P('dp'), may hold values from -6 to 6
- weight_grad: bfloat16 [8, 5120, 8192], P('section', None, 'dp'), may hold values from -6 to 6
- sweeps: int32 [8, 52], P('section'), may hold values from 1 to 4
Outputs:
- update: bfloat16 [8, 5120, 8192], P('section', None, 'dp')
Inputs may be any that keep to these rules, and one draw needn't show every extreme that they name: sweeps[s, k] is the number of Newton-Schulz iterations of block k of layer s; every value from 1 to 4 occurs.
All inputs are finite; a program needn't handle non-finite values. Where the computation divides by a largest or mean magnitude, that divisor is 1e-20 or more.
Results may differ from a plain program's by a relative error of at most 0.0067.
Values may be sent and summed in bfloat16 or wider, within the bound.
A program may use at most 128 MiB of HBM per device.

v0:
```python
import jax
import jax.numpy as jnp
from jax import lax
from jax.sharding import PartitionSpec as P

BLOCK = 256
damping = 0.05


def passed_along(block, axis, distance):
    devices = range(lax.axis_size(axis))
    route = [(i - distance, i) for i in devices if i - distance in devices]
    return lax.ppermute(block, axis, route)


def newton_single(matrix, count):
    eye = jnp.eye(matrix.shape[0], dtype=jnp.float32)
    scale = 1.0 / jnp.max(jnp.sum(jnp.abs(matrix), axis=1))

    def sweep(turn, approx):
        inner = 2.0 * eye - jnp.dot(matrix, approx, precision=lax.Precision.HIGHEST)
        return jnp.dot(approx, inner, precision=lax.Precision.HIGHEST)

    return lax.fori_loop(0, count, sweep, scale * eye)


def on_device(acts, input_grads, head_grads, weight_grad, sweeps):
    dp_count = lax.axis_size("dp")
    owner_index = lax.axis_index("dp")
    section_count = lax.axis_size("section")
    section_index = lax.axis_index("section")
    arrived = passed_along(input_grads, "section", -1)
    grads = jnp.where(section_index == section_count - 1, head_grads[None], arrived)[0]
    inputs = acts[0]
    tokens_here = inputs.shape[0]
    hidden_blocks = inputs.shape[1] // BLOCK
    model_blocks = grads.shape[1] // BLOCK
    shaped_a = inputs.reshape(tokens_here, hidden_blocks, BLOCK)
    shaped_g = grads.reshape(tokens_here, model_blocks, BLOCK)
    part_a = jnp.einsum("tkb,tkc->kbc", shaped_a, shaped_a, preferred_element_type=jnp.float32)
    part_g = jnp.einsum("tkb,tkc->kbc", shaped_g, shaped_g, preferred_element_type=jnp.float32)
    partial_value = jnp.concatenate([part_a, part_g], axis=0)
    block_count = partial_value.shape[0]
    capacity = -(-block_count // dp_count)
    slot_total = dp_count * capacity
    counts = sweeps[0]
    block_ids = jnp.arange(block_count, dtype=jnp.int32)
    ordering = jnp.argsort(-counts, stable=True)
    rank_of = jnp.argsort(ordering, stable=True)
    rounds = rank_of // dp_count
    within = rank_of % dp_count
    owner_of = jnp.where(rounds % 2 == 0, within, dp_count - 1 - within)
    slot_of = owner_of * capacity + rounds
    slot_ids = jnp.arange(slot_total, dtype=jnp.int32)
    matches = slot_of[None, :] == slot_ids[:, None]
    block_of = jnp.sum(jnp.where(matches, block_ids[None, :] + 1, 0), axis=1) - 1
    block_of = jnp.where(block_of < 0, block_count, block_of)
    my_blocks = lax.dynamic_slice_in_dim(block_of, owner_index * capacity, capacity)
    zero_block = jnp.zeros((1, BLOCK, BLOCK), jnp.float32)
    outgoing = jnp.take(jnp.concatenate([partial_value, zero_block], axis=0), block_of, axis=0)
    mine = lax.psum_scatter(outgoing, "dp", scatter_dimension=0, tiled=True)
    eye = jnp.eye(BLOCK, dtype=jnp.float32)
    factor = mine / (tokens_here * dp_count) + damping * eye[None]
    padded_counts = jnp.concatenate([counts, jnp.zeros((1,), jnp.int32)])
    my_counts = jnp.take(padded_counts, my_blocks)
    inverted = []
    for position in range(capacity):
        inverted.append(newton_single(factor[position], my_counts[position]))
    inverse = jnp.stack(inverted).astype(jnp.bfloat16)
    every_inverse = lax.all_gather(inverse, "dp", axis=0, tiled=True)
    column_count = weight_grad.shape[2]
    local_blocks = column_count // BLOCK
    column_blocks = owner_index * local_blocks + jnp.arange(local_blocks, dtype=jnp.int32)
    inverse_a = jnp.take(every_inverse, jnp.take(slot_of, column_blocks), axis=0)
    inverse_g = jnp.take(every_inverse, slot_of[hidden_blocks:], axis=0)
    weights = weight_grad[0].reshape(grads.shape[1], local_blocks, BLOCK)
    half = jnp.einsum(
        "dkb,kbc->dkc", weights, inverse_a, preferred_element_type=jnp.float32
    ).astype(jnp.bfloat16)
    half = half.reshape(model_blocks, BLOCK, column_count)
    update = jnp.einsum("kab,kbc->kac", inverse_g, half, preferred_element_type=jnp.float32)
    return update.reshape(grads.shape[1], column_count).astype(jnp.bfloat16)[None]


def solution(mesh):
    return jax.shard_map(
        on_device,
        mesh=mesh,
        in_specs=(
            P("section", "dp", None),
            P("section", "dp", None),
            P("dp", None),
            P("section", None, "dp"),
            P("section", None),
        ),
        out_specs=P("section", None, "dp"),
        check_vma=False,
    )
```

profile of v0, /device:TPU:1, one launch (start us, length us, event | category | flops | bytes accessed | tf_op | source)
XLA Modules:
  0.0 425.9 jit_solution(5902779405749802226)
XLA Ops:
  6.5 6.3 %copy.39 = bf16[1,384,5120]{1,2,0:T(8,128)(2,1)} copy(bf16[1,384,5120]{2,1,0:T(8,128)(2,1)} %param.14) | data formatting | bytes 7864320 | tf_op args[1]
  12.8 1.3 collective-permute-start
  14.1 6.3 %copy.38 = bf16[384,5120]{0,1:T(8,128)(2,1)} copy(bf16[384,5120]{1,0:T(8,128)(2,1)} %param.15) | data formatting | bytes 7864320 | tf_op args[2]
  20.4 7.6 %copy.52 = bf16[48,8,32,256]{3,2,1,0:T(8,128)(2,1)} copy(bf16[48,8,32,256]{3,1,2,0:T(8,128)(2,1)} %bitcast.126) | data formatting | bytes 12582912
  28.0 2.1 sort.31
  30.1 2.1 sort.32
  32.4 18.6 %fusion.9 = f32[32,256,256]{2,1,0:T(8,128)S(1)} fusion(bf16[384,32,256]{2,1,0:T(8,128)(2,1)} %bitcast.125), kind=kOutput, calls=%fused_computation.25 | convolution fusion | flops 1610612736 | bytes 14680064 | tf_op jit(solution)/shard_map/tkb,tkc->kbc/dot_general | solution.py:40
  51.0 50.3 %collective-permute-done = bf16[1,384,5120]{1,2,0:T(8,128)(2,1)} collective-permute-done((bf16[1,384,5120]{1,2,0:T(8,128)(2,1)}, bf16[1,384,5120]{1,2,0:T(8,128)(2,1)}, u32[]{:S(2)}, u32[]{:S(2)}) %collective-permute-start) | collective-permute-done | bytes 3932192 | tf_op jit(solution)/shard_map/ppermute | solution.py:13
  101.3 3.8 bitcast_select_fusion
  105.1 1.5 fusion.35
  106.6 5.2 %maximum_maximum_fusion = f32[53,256,256]{2,1,0:T(8,128)} fusion(f32[20,256,256]{2,1,0:T(8,128)S(1)} %fusion.35, f32[32,256,256]{2,1,0:T(8,128)S(1)} %fusion.9, f32[53]{0:T(128)S(1)} %pad.8.clone), kind=kLoop, calls=%fused_computation.21 | loop fusion | flops 6946816 | bytes 27525332 | tf_op jit(solution)/shard_map/concatenate | solution.py:60
  111.8 13.7 %gather_fusion = f32[64,256,256]{2,1,0:T(8,128)} fusion(f32[53,256,256]{2,1,0:T(8,128)} %maximum_maximum_fusion, s32[1024]{0:T(1024)S(1)} %pad_clamp_fusion.4), kind=kCustom, calls=%fused_computation | custom fusion | bytes 33554688 | tf_op jit(solution)/shard_map/jit(_take)/gather | solution.py:60
  125.5 11.6 %broadcast_select_fusion = f32[64,256,256]{2,1,0:T(8,128)} fusion(f32[64,256,256]{2,1,0:T(8,128)} %gather_fusion, pred[64]{0:T(512)(128)(4,1)S(1)} %compare_and_fusion.1), kind=kLoop, calls=%fused_computation.22 | loop fusion | flops 4194304 | bytes 33554496 | tf_op jit(solution)/shard_map/jit(_take)/select_n | solution.py:60
  137.5 0.6 gather_fusion.1
  138.2 0.7 fusion.34
  138.9 148.8 %reduce-scatter.2.cloned.1.call-done = f32[4,256,256]{2,1,0:T(8,128)} async-done(((f32[64,256,256]{2,1,0:T(8,128)}), f32[4,256,256]{2,1,0:T(8,128)}) %reduce-scatter.2.cloned.1.call-update) | async-done | bytes 1048592 | tf_op jit(solution)/shard_map/reduce_scatter | solution.py:61
  287.7 1.3 multiply_add_fusion
  289.3 0.7 reduce_max.36
  290.8 7.0 %while.44 = (s32[]{:T(128)}, f32[256,256]{0,1:T(8,128)S(1)}, s32[]{:T(128)}, f32[256,256]{1,0:T(8,128)S(1)}, s32[]{:T(128)}) while((s32[]{:T(128)}, f32[256,256]{0,1:T(8,128)S(1)}, s32[]{:T(128)}, f32[256,256]{1,0:T(8,128)S(1)}, s32[]{:T(128)}) %tuple.89), condition=%wide.region_7.8_spmd.clone, body=%wide.region_6.7_spmd.clone.sunk | while | flops 402849792 | bytes 2097213 | solution.py:24
  291.4 0.4 convolution_subtract_fusion.8
  291.8 0.6 convolution_bitcast_fusion.8
  293.0 0.4 convolution_subtract_fusion.8
  293.4 0.6 convolution_bitcast_fusion.8
  294.6 0.4 convolution_subtract_fusion.8
  295.0 0.6 convolution_bitcast_fusion.8
  296.6 0.6 convolution_bitcast_fusion.8
  297.9 0.7 reduce_max.37
  299.4 5.7 %while.45 = (s32[]{:T(128)}, f32[256,256]{0,1:T(8,128)S(1)}, s32[]{:T(128)}, f32[256,256]{1,0:T(8,128)S(1)}, s32[]{:T(128)}) while((s32[]{:T(128)}, f32[256,256]{0,1:T(8,128)S(1)}, s32[]{:T(128)}, f32[256,256]{1,0:T(8,128)S(1)}, s32[]{:T(128)}) %tuple.86), condition=%wide.region_11.12_spmd.clone, body=%wide.region_10.11_spmd.clone.sunk | while | flops 402849792 | bytes 2097213 | solution.py:24
  300.0 0.4 convolution_subtract_fusion.9
  300.5 0.6 convolution_bitcast_fusion.9
  302.2 0.6 convolution_bitcast_fusion.9
  303.9 0.6 convolution_bitcast_fusion.9
  305.2 0.7 reduce_max.38
  306.6 4.4 %while.46 = (s32[]{:T(128)}, f32[256,256]{0,1:T(8,128)S(1)}, s32[]{:T(128)}, f32[256,256]{1,0:T(8,128)S(1)}, s32[]{:T(128)}) while((s32[]{:T(128)}, f32[256,256]{0,1:T(8,128)S(1)}, s32[]{:T(128)}, f32[256,256]{1,0:T(8,128)S(1)}, s32[]{:T(128)}) %tuple.83), condition=%wide.region_15.16_spmd.clone, body=%wide.region_14.15_spmd.clone.sunk | while | flops 402849792 | bytes 2097213 | solution.py:24
  307.8 0.6 convolution_bitcast_fusion.10
  309.1 0.4 convolution_subtract_fusion.10
  309.5 0.6 convolution_bitcast_fusion.10
  311.2 0.7 reduce_max.39
  312.6 0.6 while.47
  313.3 0.9 pad_maximum_fusion
  314.3 0.6 gather_fusion.3
  314.9 8.3 %reshape_squeeze.11 = bf16[5120,2,256]{2,1,0:T(2,128)(2,1)} reshape(bf16[1,5120,512]{2,1,0:T(8,128)(2,1)} %param.16) | data formatting | bytes 10485760 | tf_op jit(solution)/shard_map/reshape;squeeze | solution.py:76
  323.3 64.0 %all-gather.2.cloned.1.call-done = bf16[64,256,256]{2,1,0:T(8,128)(2,1)} async-done(((bf16[4,256,256]{2,1,0:T(8,128)(2,1)}), bf16[64,256,256]{2,1,0:T(8,128)(2,1)}) %all-gather.2.cloned.1.call-update) | async-done | bytes 8388624 | tf_op jit(solution)/shard_map/all_gather | solution.py:70
  387.3 3.9 gather_fusion.4
  391.2 6.5 %fusion.8 = bf16[5120,2,256]{0,2,1:T(8,128)(2,1)} fusion(bf16[5120,2,256]{2,1,0:T(2,128)(2,1)} %reshape_squeeze.11, bf16[2,256,256]{2,1,0:T(8,128)(2,1)S(1)} %gather_fusion.4, pred[2]{0:T(512)(128)(4,1)S(1)} %compare_and_fusion), kind=kOutput, calls=%fused_computation.24 | convolution fusion | flops 1344929792 | bytes 10747906 | tf_op jit(solution)/shard_map/dkb,kbc->dkc/dot_general | solution.py:77
  397.7 10.0 %reshape.165 = bf16[20,256,512]{1,0,2:T(8,128)(2,1)} reshape(bf16[5120,2,256]{0,2,1:T(8,128)(2,1)} %fusion.8) | data formatting | bytes 10485760 | tf_op jit(solution)/shard_map/reshape | solution.py:80
  407.7 4.1 gather_fusion.2
  411.8 7.2 %fusion.14 = bf16[20,256,512]{2,1,0:T(8,128)(2,1)} fusion(bf16[20,256,512]{1,0,2:T(8,128)(2,1)} %reshape.165, bf16[20,256,256]{2,1,0:T(8,128)(2,1)S(1)} %gather_fusion.2, pred[20]{0:T(512)(128)(4,1)S(1)} %get-tuple-element.205), kind=kOutput, calls=%fused_computation.31 | convolution fusion | flops 1346109440 | bytes 13107220 | tf_op jit(solution)/shard_map/kab,kbc->kac/dot_general | solution.py:81
  (52 shorter events, 3.4 us)
Async XLA Ops:
  6.5 281.1 %reduce-scatter.2.cloned.1.call-start = ((), (), s32[]{:S(2)}) async-start(), calls=%async_computation.1 | async-start | bytes 17825792 | tf_op jit(solution)/shard_map/reduce_scatter | solution.py:61
  12.8 88.5 %collective-permute-start = (bf16[1,384,5120]{1,2,0:T(8,128)(2,1)}, bf16[1,384,5120]{1,2,0:T(8,128)(2,1)}, u32[]{:S(2)}, u32[]{:S(2)}) collective-permute-start(bf16[1,384,5120]{1,2,0:T(8,128)(2,1)} %copy.39), channel_id=1, source_target_pairs={{16,0},{32,16},{48,32},{64,48},{80,64},{96,80},{112,96},{17,1},{33... | collective-permute-start | bytes 11796488 | tf_op jit(solution)/shard_map/ppermute | solution.py:13
  20.4 7.6 %copy-start = (s32[1,52]{1,0:T(1,128)S(1)}, s32[1,52]{1,0:T(1,128)}, u32[]{:S(2)}) copy-start(s32[1,52]{1,0:T(1,128)} %param.17) | copy-start | bytes 628
  137.1 250.2 %all-gather.2.cloned.1.call-start = ((), (), s32[]{:S(2)}) async-start(), calls=%async_computation.2 | async-start | bytes 8912896 | tf_op jit(solution)/shard_map/all_gather | solution.py:70
Sparse Core Ops, SparseCore 0:
  137.2 150.3 reduce-scatter.1
  314.4 72.8 all-gather.1
where the time goes:
time: 427 us; the launch traced here: 426 us
  waiting for transfers between devices  263 us (62%)
  local copies, waits for them, and re-layouts  62.9 us (15%)
  matrix products  43 us (10%)
  other arithmetic  30.5 us (7%)
  between operations  16.6 us (4%)
  loops' own time  8.52 us (2%)
    reduce_scatter x1, waiting for transfers between devices, on_device(): mine = lax.psum_scatter(outgoing, 'dp', scatter_dimension=0, tiled=True)  149 us
    all_gather x1, waiting for transfers between devices, on_device(): every_inverse = lax.all_gather(inverse, 'dp', axis=0, tiled=True)  64 us
    ppermute x1, waiting for transfers between devices, passed_along(): return lax.ppermute(block, axis, route)  50.3 us
    unnamed x5, local copies, waits for them, and re-layouts  20.1 us
    dot_general x1, matrix products, on_device(): jnp.einsum('tkb,tkc->kbc', shaped_a, shaped_a, preferred_element_type=jnp...  18.6 us
    gather x1, local copies, waits for them, and re-layouts, on_device(): jnp.take(jnp.concatenate([partial_value, zero_block], axis=0), block_of,...  13.7 us
    select_n x2, other arithmetic, on_device(): jnp.take(jnp.concatenate([partial_value, zero_block], axis=0), block_of,...  11.6 us
    reshape x1, local copies, waits for them, and re-layouts, on_device(): half = half.reshape(model_blocks, BLOCK, column_count)  9.95 us
  transfers between devices with their start and end apart: 3, of which 3 were waited for; matrix products, arithmetic and copies ran while one was open for 11% of the time, Pallas kernels for 0%

commit v1 on v0

--- a/solution.py
+++ b/solution.py
@@ -67,7 +67,10 @@
     for position in range(capacity):
         inverted.append(newton_single(factor[position], my_counts[position]))
     inverse = jnp.stack(inverted).astype(jnp.bfloat16)
-    every_inverse = lax.all_gather(inverse, "dp", axis=0, tiled=True)
+    size = lax.axis_size("dp")
+    blocks = jnp.stack([inverse for _ in range(size)])
+    blocks = lax.all_to_all(blocks, "dp", split_axis=0, concat_axis=0)
+    every_inverse = jnp.concatenate(blocks, axis=0)
     column_count = weight_grad.shape[2]
     local_blocks = column_count // BLOCK
     column_blocks = owner_index * local_blocks + jnp.arange(local_blocks, dtype=jnp.int32)

time: 427 us -> 491 us (1.15); the launches traced: 426 us -> 483 us
  waiting for transfers between devices: 263 us -> 313 us
    all_to_all x0 -> x1, waiting for transfers between devices: none -> 114 us  [on_device(): blocks = lax.all_to_all(blocks, 'dp', split_axis=0, concat_axis=0)]
    all_gather x1 -> x0, waiting for transfers between devices: 64 us -> none  [on_device(): every_inverse = lax.all_gather(inverse, 'dp', axis=0, tiled=True)]
  transfers between devices with their start and end apart: 3 -> 3, of which waited for: 3 -> 3; matrix products, arithmetic and copies ran while one was open for 11% -> 10% of each run, Pallas kernels for 0% -> 0%
where the time goes in v1:
time: 491 us; the launch traced here: 483 us
  waiting for transfers between devices  313 us (64%)
  local copies, waits for them, and re-layouts  67 us (14%)
  matrix products  43 us (9%)
  other arithmetic  29.7 us (6%)
  between operations  16.6 us (3%)
  loops' own time  8.52 us (2%)
  starting transfers between devices  5.94 us (1%)
    reduce_scatter x1, waiting for transfers between devices, on_device(): mine = lax.psum_scatter(outgoing, 'dp', scatter_dimension=0, tiled=True)  149 us
    all_to_all x1, waiting for transfers between devices, on_device(): blocks = lax.all_to_all(blocks, 'dp', split_axis=0, concat_axis=0)  114 us
    ppermute x1, waiting for transfers between devices, passed_along(): return lax.ppermute(block, axis, route)  50.3 us
    unnamed x5, local copies, waits for them, and re-layouts  20.1 us
    dot_general x1, matrix products, on_device(): jnp.einsum('tkb,tkc->kbc', shaped_a, shaped_a, preferred_element_type=jnp...  18.6 us
    gather x1, local copies, waits for them, and re-layouts, on_device(): jnp.take(jnp.concatenate([partial_value, zero_block], axis=0), block_of,...  13.7 us
    select_n x2, other arithmetic, on_device(): jnp.take(jnp.concatenate([partial_value, zero_block], axis=0), block_of,...  11.6 us
    reshape x1, local copies, waits for them, and re-layouts, on_device(): half = half.reshape(model_blocks, BLOCK, column_count)  9.95 us
  transfers between devices with their start and end apart: 3, of which 3 were waited for; matrix products, arithmetic and copies ran while one was open for 10% of the time, Pallas kernels for 0%

profile of v1, /device:TPU:1, one launch (start us, length us, event | category | flops | bytes accessed | tf_op | source)
XLA Modules:
  0.0 483.4 jit_solution(2079807146512385781)
XLA Ops:
  6.5 6.3 %copy.27 = bf16[1,384,5120]{1,2,0:T(8,128)(2,1)} copy(bf16[1,384,5120]{2,1,0:T(8,128)(2,1)} %param.14) | data formatting | bytes 7864320 | tf_op args[1]
  12.8 1.3 collective-permute-start
  14.1 6.3 %copy.26 = bf16[384,5120]{0,1:T(8,128)(2,1)} copy(bf16[384,5120]{1,0:T(8,128)(2,1)} %param.15) | data formatting | bytes 7864320 | tf_op args[2]
  20.4 7.6 %copy.37 = bf16[48,8,32,256]{3,2,1,0:T(8,128)(2,1)} copy(bf16[48,8,32,256]{3,1,2,0:T(8,128)(2,1)} %bitcast.123) | data formatting | bytes 12582912
  28.0 2.1 sort.31
  30.1 2.1 sort.32
  32.4 18.6 %fusion.9 = f32[32,256,256]{2,1,0:T(8,128)S(1)} fusion(bf16[384,32,256]{2,1,0:T(8,128)(2,1)} %bitcast.122), kind=kOutput, calls=%fused_computation.25 | convolution fusion | flops 1610612736 | bytes 14680064 | tf_op jit(solution)/shard_map/tkb,tkc->kbc/dot_general | solution.py:40
  51.0 50.3 %collective-permute-done = bf16[1,384,5120]{1,2,0:T(8,128)(2,1)} collective-permute-done((bf16[1,384,5120]{1,2,0:T(8,128)(2,1)}, bf16[1,384,5120]{1,2,0:T(8,128)(2,1)}, u32[]{:S(2)}, u32[]{:S(2)}) %collective-permute-start) | collective-permute-done | bytes 3932192 | tf_op jit(solution)/shard_map/ppermute | solution.py:13
  101.3 3.8 bitcast_select_fusion
  105.1 1.5 fusion.35
  106.6 5.2 %maximum_maximum_fusion = f32[53,256,256]{2,1,0:T(8,128)} fusion(f32[20,256,256]{2,1,0:T(8,128)S(1)} %fusion.35, f32[32,256,256]{2,1,0:T(8,128)S(1)} %fusion.9, f32[53]{0:T(128)S(1)} %pad.8.clone), kind=kLoop, calls=%fused_computation.21 | loop fusion | flops 6946816 | bytes 27525332 | tf_op jit(solution)/shard_map/concatenate | solution.py:60
  111.8 13.7 %gather_fusion = f32[64,256,256]{2,1,0:T(8,128)} fusion(f32[53,256,256]{2,1,0:T(8,128)} %maximum_maximum_fusion, s32[1024]{0:T(1024)S(1)} %pad_clamp_fusion.4), kind=kCustom, calls=%fused_computation | custom fusion | bytes 33554688 | tf_op jit(solution)/shard_map/jit(_take)/gather | solution.py:60
  125.5 11.6 %broadcast_select_fusion = f32[64,256,256]{2,1,0:T(8,128)} fusion(f32[64,256,256]{2,1,0:T(8,128)} %gather_fusion, pred[64]{0:T(512)(128)(4,1)S(1)} %compare_and_fusion.1), kind=kLoop, calls=%fused_computation.22 | loop fusion | flops 4194304 | bytes 33554496 | tf_op jit(solution)/shard_map/jit(_take)/select_n | solution.py:60
  137.5 0.6 gather_fusion.1
  138.2 0.7 fusion.34
  138.9 148.8 %reduce-scatter.2.cloned.1.call-done = f32[4,256,256]{2,1,0:T(8,128)} async-done(((f32[64,256,256]{2,1,0:T(8,128)}), f32[4,256,256]{2,1,0:T(8,128)}) %reduce-scatter.2.cloned.1.call-update) | async-done | bytes 1048592 | tf_op jit(solution)/shard_map/reduce_scatter | solution.py:61
  287.7 1.3 multiply_add_fusion
  289.3 0.7 reduce_max.36
  290.8 7.0 %while.44 = (s32[]{:T(128)}, f32[256,256]{0,1:T(8,128)S(1)}, s32[]{:T(128)}, f32[256,256]{1,0:T(8,128)S(1)}, s32[]{:T(128)}) while((s32[]{:T(128)}, f32[256,256]{0,1:T(8,128)S(1)}, s32[]{:T(128)}, f32[256,256]{1,0:T(8,128)S(1)}, s32[]{:T(128)}) %tuple.89), condition=%wide.region_7.8_spmd.clone, body=%wide.region_6.7_spmd.clone.sunk | while | flops 402849792 | bytes 2097213 | solution.py:24
  291.8 0.6 convolution_bitcast_fusion.8
  293.0 0.4 convolution_subtract_fusion.8
  293.4 0.6 convolution_bitcast_fusion.8
  294.6 0.4 convolution_subtract_fusion.8
  295.0 0.6 convolution_bitcast_fusion.8
  296.6 0.6 convolution_bitcast_fusion.8
  297.8 0.7 reduce_max.37
  299.3 5.7 %while.45 = (s32[]{:T(128)}, f32[256,256]{0,1:T(8,128)S(1)}, s32[]{:T(128)}, f32[256,256]{1,0:T(8,128)S(1)}, s32[]{:T(128)}) while((s32[]{:T(128)}, f32[256,256]{0,1:T(8,128)S(1)}, s32[]{:T(128)}, f32[256,256]{1,0:T(8,128)S(1)}, s32[]{:T(128)}) %tuple.86), condition=%wide.region_11.12_spmd.clone, body=%wide.region_10.11_spmd.clone.sunk | while | flops 402849792 | bytes 2097213 | solution.py:24
  300.0 0.4 convolution_subtract_fusion.9
  300.4 0.6 convolution_bitcast_fusion.9
  302.1 0.6 convolution_bitcast_fusion.9
  303.4 0.4 convolution_subtract_fusion.9
  303.8 0.6 convolution_bitcast_fusion.9
  305.0 0.7 reduce_max.38
  306.5 4.4 while.46
  307.6 0.6 convolution_bitcast_fusion.10
  309.4 0.6 convolution_bitcast_fusion.10
  310.9 0.7 reduce_max.39
  312.4 0.6 while.47
  313.3 4.2 stack.17
  317.5 4.7 all-to-all-start
  322.2 0.6 gather_fusion.3
  322.8 8.3 %reshape_squeeze.11 = bf16[5120,2,256]{2,1,0:T(2,128)(2,1)} reshape(bf16[1,5120,512]{2,1,0:T(8,128)(2,1)} %param.16) | data formatting | bytes 10485760 | tf_op jit(solution)/shard_map/reshape;squeeze | solution.py:79
  331.2 113.6 %all-to-all-done = bf16[16,4,256,256]{3,2,1,0:T(8,128)(2,1)} async-done(((bf16[16,4,256,256]{3,2,1,0:T(8,128)(2,1)}), bf16[16,4,256,256]{3,2,1,0:T(8,128)(2,1)}, u32[]{:S(2)}, u32[]{:S(2)}) %all-to-all-start) | async-done | bytes 8388640 | tf_op jit(solution)/shard_map/all_to_all | solution.py:72
  444.8 3.9 gather_fusion.4
  448.8 6.5 %fusion.8 = bf16[5120,2,256]{0,2,1:T(8,128)(2,1)} fusion(bf16[5120,2,256]{2,1,0:T(2,128)(2,1)} %reshape_squeeze.11, bf16[2,256,256]{2,1,0:T(8,128)(2,1)S(1)} %gather_fusion.4, pred[2]{0:T(512)(128)(4,1)S(1)} %compare_and_fusion), kind=kOutput, calls=%fused_computation.24 | convolution fusion | flops 1344929792 | bytes 10747906 | tf_op jit(solution)/shard_map/dkb,kbc->dkc/dot_general | solution.py:80
  455.3 10.0 %reshape.190 = bf16[20,256,512]{1,0,2:T(8,128)(2,1)} reshape(bf16[5120,2,256]{0,2,1:T(8,128)(2,1)} %fusion.8) | data formatting | bytes 10485760 | tf_op jit(solution)/shard_map/reshape | solution.py:83
  465.2 4.1 gather_fusion.2
  469.3 7.2 %fusion.14 = bf16[20,256,512]{2,1,0:T(8,128)(2,1)} fusion(bf16[20,256,512]{1,0,2:T(8,128)(2,1)} %reshape.190, bf16[20,256,256]{2,1,0:T(8,128)(2,1)S(1)} %gather_fusion.2, pred[20]{0:T(512)(128)(4,1)S(1)} %get-tuple-element.205), kind=kOutput, calls=%fused_computation.31 | convolution fusion | flops 1346109440 | bytes 13107220 | tf_op jit(solution)/shard_map/kab,kbc->kac/dot_general | solution.py:84
  (53 shorter events, 3.7 us)
Async XLA Ops:
  6.5 281.1 %reduce-scatter.2.cloned.1.call-start = ((), (), s32[]{:S(2)}) async-start(), calls=%async_computation.2 | async-start | bytes 17825792 | tf_op jit(solution)/shard_map/reduce_scatter | solution.py:61
  12.8 88.5 %collective-permute-start = (bf16[1,384,5120]{1,2,0:T(8,128)(2,1)}, bf16[1,384,5120]{1,2,0:T(8,128)(2,1)}, u32[]{:S(2)}, u32[]{:S(2)}) collective-permute-start(bf16[1,384,5120]{1,2,0:T(8,128)(2,1)} %copy.27), channel_id=1, source_target_pairs={{16,0},{32,16},{48,32},{64,48},{80,64},{96,80},{112,96},{17,1},{33... | collective-permute-start | bytes 11796488 | tf_op jit(solution)/shard_map/ppermute | solution.py:13
  20.4 7.6 %copy-start = (s32[1,52]{1,0:T(1,128)S(1)}, s32[1,52]{1,0:T(1,128)}, u32[]{:S(2)}) copy-start(s32[1,52]{1,0:T(1,128)} %param.17) | copy-start | bytes 628
  317.5 127.3 %all-to-all-start = ((bf16[16,4,256,256]{3,2,1,0:T(8,128)(2,1)}), bf16[16,4,256,256]{3,2,1,0:T(8,128)(2,1)}, u32[]{:S(2)}, u32[]{:S(2)}) async-start(bf16[16,4,256,256]{3,2,1,0:T(8,128)(2,1)} %stack.17), calls=%async_computation.1 | async-start | bytes 16777216 | tf_op jit(solution)/shard_map/all_to_all | solution.py:72
Sparse Core Ops, SparseCore 0:
  137.2 150.3 reduce-scatter.1
